TPU v7x, 32 devices: a whole 2x2x4 slice. The times are simulated.
32 devices in a mesh: px: 2 (over core), pz: 16 (over z, y, x).
Axes of the slice: x: 2, y: 2, z: 4, core: 2. Of those that a mesh axis runs over, the one named last changes fastest.
Arguments:
- velocity: float32 [3, 256, 32, 256], P(None, 'pz', None, 'px'), may hold values from -8 to 8, as said below
- filter_inverse: float32 [256, 256], replicated, may hold values from 0 to 2, as said below
- filter_block: int32 [256], replicated, may hold values from 0 to 7, never falling along the last dimension, each value on 1 to 128 neighbouring positions
- plane_bin: int32 [256], replicated, may hold values from 0 to 63, never falling along the last dimension, each value on 1 to 16 neighbouring positions
Outputs:
- leonard: float32 [6, 256, 32, 256], P(None, 'pz', None, 'px')
- viscosity: float32 [256, 32, 256], P('pz', None, 'px')
- coefficient: float32 [256], replicated
Inputs may be any that keep to these rules, and one draw needn't show every extreme that they name: `velocity`: each component is a rough random field. `filter_inverse`: entries are positive. `filter_block`: never falls along the planes; each of the 8 blocks holds 1 to 128 consecutive planes, one exactly 128. `plane_bin`: never falls along the planes; each of the 64 bins holds 1 to 16 consecutive planes, one exactly 16.
All inputs are finite; a program needn't handle non-finite values.
Results may differ from a plain program's by a relative error of at most 0.0003.
Values sent between devices are 32-bit elements; how exact they have to be, the bound alone decides.
A program may use at most 128 MiB of HBM per device.

v0:
```python
import jax
import jax.numpy as jnp
from jax import lax
from jax.sharding import PartitionSpec as P

NBIN = 64


def with_halo(cells, sides, width, closed):
    for axis, dim in sides:
        count = lax.axis_size(axis)
        ends = count if closed else count - 1
        head = lax.slice_in_dim(cells, 0, width, axis=dim)
        tail = lax.slice_in_dim(cells, cells.shape[dim] - width, cells.shape[dim], axis=dim)
        cells = jnp.concatenate(
            [
                lax.ppermute(tail, axis, [(i, (i + 1) % count) for i in range(ends)]),
                cells,
                lax.ppermute(head, axis, [((i + 1) % count, i) for i in range(ends)]),
            ],
            axis=dim,
        )
    return cells


def quantities(padded):
    centre = padded[:, 1:-1, 1:-1, 1:-1]
    along_y = (padded[:, 2:, 1:-1, 1:-1] - padded[:, :-2, 1:-1, 1:-1]) * 0.5
    along_z = (padded[:, 1:-1, 2:, 1:-1] - padded[:, 1:-1, :-2, 1:-1]) * 0.5
    along_x = (padded[:, 1:-1, 1:-1, 2:] - padded[:, 1:-1, 1:-1, :-2]) * 0.5
    strain = jnp.stack(
        [
            along_x[0],
            along_y[1],
            along_z[2],
            0.5 * (along_y[0] + along_x[1]),
            0.5 * (along_z[0] + along_x[2]),
            0.5 * (along_z[1] + along_y[2]),
        ]
    )
    magnitude = jnp.sqrt(
        2.0 * jnp.sum(strain[:3] * strain[:3], axis=0)
        + 4.0 * jnp.sum(strain[3:] * strain[3:], axis=0)
    )
    products = jnp.stack(
        [
            centre[0] * centre[0],
            centre[1] * centre[1],
            centre[2] * centre[2],
            centre[0] * centre[1],
            centre[0] * centre[2],
            centre[1] * centre[2],
        ]
    )
    fields = jnp.concatenate([centre, strain, products, magnitude[None] * strain], axis=0)
    along = (fields[..., :-2] + 2.0 * fields[..., 1:-1] + fields[..., 2:]) * 0.25
    boxed = (along[:, :, :-2] + 2.0 * along[:, :, 1:-1] + along[:, :, 2:]) * 0.25
    return (boxed, magnitude[:, 1:-1, 1:-1])


def contract(filtered):
    speed = filtered[0:3]
    strain = filtered[3:9]
    products = filtered[9:15]
    scaled = filtered[15:21]
    leonard = products - jnp.stack(
        [
            speed[0] * speed[0],
            speed[1] * speed[1],
            speed[2] * speed[2],
            speed[0] * speed[1],
            speed[0] * speed[2],
            speed[1] * speed[2],
        ]
    )
    fmag = jnp.sqrt(
        2.0 * jnp.sum(strain[:3] * strain[:3], axis=0)
        + 4.0 * jnp.sum(strain[3:] * strain[3:], axis=0)
    )
    model = scaled - 4.0 * fmag[None] * strain
    weights = jnp.array([1.0, 1.0, 1.0, 2.0, 2.0, 2.0], jnp.float32).reshape(6, 1, 1, 1)
    product_lm = jnp.sum(weights * leonard * model, axis=0)
    product_mm = jnp.sum(weights * model * model, axis=0)
    return (leonard, product_lm, product_mm)


def local(velocity, filter_inverse, filter_block, plane_bin):
    same = (filter_block[:, None] == filter_block[None, :]).astype(jnp.float32)
    masked = filter_inverse * same
    weights = masked / jnp.sum(masked, axis=1, keepdims=True)
    local_planes = velocity.shape[1]
    extended = with_halo(velocity, (("px", 3),), 2, True)
    extended = with_halo(extended, (("pz", 1),), 1, False)
    extended = jnp.concatenate([extended[:, :, -2:], extended, extended[:, :, :2]], axis=2)
    boxed, magnitude = quantities(extended)
    smooth_boxed = lax.all_to_all(boxed, "pz", split_axis=2, concat_axis=1, tiled=True)
    filtered = jnp.einsum("ab,kbzx->kazx", weights, smooth_boxed, precision=lax.Precision.HIGHEST)
    leonard, product_lm, product_mm = contract(filtered)
    onehot = (plane_bin[:, None] == jnp.arange(NBIN, dtype=jnp.int32)[None, :]).astype(jnp.float32)
    local_lm = jnp.dot(jnp.sum(product_lm, axis=(1, 2)), onehot, precision=lax.Precision.HIGHEST)
    local_mm = jnp.dot(jnp.sum(product_mm, axis=(1, 2)), onehot, precision=lax.Precision.HIGHEST)
    numer, denom = lax.psum((local_lm, local_mm), ("px", "pz"))
    cells = filtered.shape[3] * lax.axis_size("px") * filtered.shape[2] * lax.axis_size("pz")
    per_bin = numer / jnp.maximum(denom, jnp.float32(cells))
    coefficient = jnp.dot(onehot, per_bin, precision=lax.Precision.HIGHEST)
    leonard_back = lax.all_to_all(leonard, "pz", split_axis=1, concat_axis=2, tiled=True)
    offset = lax.axis_index("pz") * local_planes
    local_coef = lax.dynamic_slice_in_dim(coefficient, offset, local_planes, 0)
    viscosity = local_coef[:, None, None] * magnitude
    return (leonard_back, viscosity, coefficient)


def solution(mesh):
    return jax.shard_map(
        local,
        mesh=mesh,
        in_specs=(P(None, "pz", None, "px"), P(), P(), P()),
        out_specs=(P(None, "pz", None, "px"), P("pz", None, "px"), P()),
        check_vma=False,
    )
```

profile of v0, /device:TPU:0, one launch (start us, length us, event | category | flops | bytes accessed | tf_op | source)
XLA Modules:
  0.0 246.9 jit_solution(18244381259723919933)
XLA Ops:
  0.6 1.7 fusion.38
  2.4 0.4 copy.41
  2.7 0.5 collective-permute-start
  3.3 0.3 copy.42
  3.7 0.5 copy.24
  4.2 0.4 copy.23
  4.6 0.3 collective-permute-done.1
  4.9 0.4 copy.25
  5.3 0.7 pad_maximum_fusion.18
  6.0 4.6 %collective-permute-start.2 = (f32[3,1,32,132]{3,1,0,2:T(1,128)S(1)}, f32[3,1,32,132]{3,1,0,2:T(1,128)S(1)}, u32[]{:S(2)}, u32[]{:S(2)}) collective-permute-start(f32[3,1,32,132]{3,1,0,2:T(1,128)S(1)} %get-tuple-element.27), channel_id=1, source_target_pairs={{0,1},{1,2},{2,3},{3,4},{4,5},{5,6},{6,7},{7,8},{8,9},{9,10},{10,1... | collective-permute-start | bytes 152072 | tf_op jit(solution)/shard_map/ppermute | solution.py:17
  10.6 1.5 collective-permute-start.3
  12.1 1.0 collective-permute-done.2
  13.1 4.1 %collective-permute-done.3 = f32[3,1,32,132]{3,1,0,2:T(1,128)S(1)} collective-permute-done((f32[3,1,32,132]{3,1,0,2:T(1,128)S(1)}, f32[3,1,32,132]{3,1,0,2:T(1,128)S(1)}, u32[]{:S(2)}, u32[]{:S(2)}) %collective-permute-start.3) | collective-permute-done | bytes 50720 | tf_op jit(solution)/shard_map/ppermute | solution.py:19
  17.2 0.2 pad_maximum_fusion.15
  17.4 1.0 pad_maximum_fusion
  18.5 3.0 %fusion.6 = (f32[3,16,34,130]{3,1,0,2:T(8,128)}, f32[3,16,34,130]{3,1,0,2:T(8,128)S(1)}, f32[21,16,34,130]{3,1,0,2:T(8,128)S(1)}) fusion(f32[3,18,36,132]{3,1,0,2:T(8,128)S(1)} %pad_maximum_fusion), kind=kLoop, calls=%fused_computation.25 | loop fusion | flops 848639 | bytes 8434176 | tf_op jit(solution)/shard_map/mul | solution.py:28
  21.6 1.2 fusion.36
  22.8 2.1 fusion.5
  25.0 0.2 fusion.37
  25.3 0.2 constant_dynamic-update-slice_fusion.1
  25.6 0.2 fusion.9
  25.9 0.2 multiply_dynamic-update-slice_fusion.6
  26.1 0.2 multiply_dynamic-update-slice_fusion.5
  26.3 0.2 multiply_dynamic-update-slice_fusion.4
  26.6 0.4 multiply_dynamic-update-slice_fusion.3
  26.9 0.4 multiply_dynamic-update-slice_fusion.2
  27.3 0.4 multiply_dynamic-update-slice_fusion.1
  27.7 0.2 fusion.8
  27.9 0.2 add_sqrt_fusion
  28.1 0.5 multiply_dynamic-update-slice_fusion
  28.7 3.2 %fusion = f32[21,16,34,128]{3,1,0,2:T(8,128)S(1)} fusion(f32[21,16,34,130]{3,1,0,2:T(8,128)S(1)} %multiply_dynamic-update-slice_fusion), kind=kLoop, calls=%fused_computation.1 | loop fusion | flops 5849088 | bytes 23396352 | tf_op jit(solution)/shard_map/mul | solution.py:56
  31.9 3.2 %fusion.2 = f32[21,16,32,128]{3,1,0,2:T(8,128)} fusion(f32[21,16,34,128]{3,1,0,2:T(8,128)S(1)} %fusion), kind=kLoop, calls=%fused_computation.5 | loop fusion | flops 5505024 | bytes 22020096 | tf_op jit(solution)/shard_map/mul | solution.py:57
  35.0 7.8 %all-to-all-start = ((f32[21,16,32,128]{3,1,0,2:T(8,128)}), f32[21,16,32,128]{3,1,0,2:T(8,128)}, u32[]{:S(2)}, u32[]{:S(2)}) async-start(f32[21,16,32,128]{3,1,0,2:T(8,128)} %fusion.2), calls=%async_computation | async-start | bytes 11010048 | tf_op jit(solution)/shard_map/all_to_all | solution.py:96
  42.9 0.2 fusion.19
  43.1 102.0 %all-to-all-done = f32[21,16,32,128]{3,1,0,2:T(8,128)} async-done(((f32[21,16,32,128]{3,1,0,2:T(8,128)}), f32[21,16,32,128]{3,1,0,2:T(8,128)}, u32[]{:S(2)}, u32[]{:S(2)}) %all-to-all-start) | async-done | bytes 5505056 | tf_op jit(solution)/shard_map/all_to_all | solution.py:96
  145.1 3.3 %copy.29 = f32[21,16,16,2,128]{4,2,1,3,0:T(8,128)S(1)} copy(f32[21,16,16,2,128]{4,2,0,3,1:T(8,128)} %bitcast.2) | data formatting | bytes 11010048 | tf_op jit(solution)/shard_map/all_to_all | solution.py:96
  148.4 8.8 %convolution_bitcast_fusion = f32[21,256,2,128]{1,3,2,0:T(8,128)S(1)} fusion(f32[21,256,2,128]{3,1,2,0:T(8,128)S(1)} %bitcast.28, f32[256,256]{1,0:T(8,128)S(1)} %copy-done.2, f32[256]{0:T(256)S(1)} %fusion.19, s32[256]{0:T(256)S(1)} %copy-done.3), kind=kOutput, calls=%fused_computation.10 | convolution fusion | flops 4228055040 | bytes 11274240 | tf_op jit(solution)/shard_map/ab,kbzx->kazx/dot_general | solution.py:97
  157.7 0.3 copy-done.4
  158.0 0.7 fusion.10
  158.7 2.1 copy.31
  160.8 25.5 %all-to-all-start.1 = ((f32[6,256,2,128]{3,2,0,1:T(2,128)}), f32[6,256,2,128]{3,2,0,1:T(2,128)S(1)}, u32[]{:S(2)}, u32[]{:S(2)}) async-start(f32[6,256,2,128]{3,2,0,1:T(2,128)} %copy.31), calls=%async_computation.1 | async-start | bytes 3145728 | tf_op jit(solution)/shard_map/all_to_all | solution.py:106
  186.3 0.2 convolution_bitcast_fusion.1
  186.6 0.2 convolution_bitcast_fusion.2
  186.8 56.8 %all-reduce = (f32[64]{0:T(128)S(1)}, f32[64]{0:T(128)S(1)}) all-reduce(f32[64]{0:T(128)S(1)} %convolution_bitcast_fusion.2, f32[64]{0:T(128)S(1)} %convolution_bitcast_fusion.1), channel_id=1, replica_groups=mesh['px'=2,'pz'=16] {'px','pz'}, use_global_device_ids=true, to_apply=%region_6.0 | all-reduce | flops 128 | bytes 1024 | tf_op jit(solution)/shard_map/psum | solution.py:102
  243.6 0.2 fusion.20
  244.1 0.8 copy.35
  245.0 0.2 copy.33
  245.2 1.6 copy.34
  (32 shorter events, 1.4 us)
Async XLA Ops:
  0.6 3.1 %copy-start = (f32[3,16,32,128]{3,2,1,0:T(8,128)S(1)}, f32[3,16,32,128]{3,2,1,0:T(8,128)}, u32[]{:S(2)}) copy-start(f32[3,16,32,128]{3,2,1,0:T(8,128)} %param.5) | copy-start | bytes 2359300
  2.7 1.4 collective-permute-start
  3.6 1.3 collective-permute-start.1
  6.0 7.1 %collective-permute-start.2 = (f32[3,1,32,132]{3,1,0,2:T(1,128)S(1)}, f32[3,1,32,132]{3,1,0,2:T(1,128)S(1)}, u32[]{:S(2)}, u32[]{:S(2)}) collective-permute-start(f32[3,1,32,132]{3,1,0,2:T(1,128)S(1)} %get-tuple-element.27), channel_id=1, source_target_pairs={{0,1},{1,2},{2,3},{3,4},{4,5},{5,6},{6,7},{7,8},{8,9},{9,10},{10,1... | collective-permute-start | bytes 152072 | tf_op jit(solution)/shard_map/ppermute | solution.py:17
  10.6 6.6 %collective-permute-start.3 = (f32[3,1,32,132]{3,1,0,2:T(1,128)S(1)}, f32[3,1,32,132]{3,1,0,2:T(1,128)S(1)}, u32[]{:S(2)}, u32[]{:S(2)}) collective-permute-start(f32[3,1,32,132]{3,1,0,2:T(1,128)S(1)} %get-tuple-element.28), channel_id=1, source_target_pairs={{1,0},{2,1},{3,2},{4,3},{5,4},{6,5},{7,6},{8,7},{9,8},{10,9},{11,1... | collective-permute-start | bytes 152072 | tf_op jit(solution)/shard_map/ppermute | solution.py:19
  22.8 2.3 copy-start.1
  35.0 7.9 %copy-start.2 = (f32[256,256]{1,0:T(8,128)S(1)}, f32[256,256]{1,0:T(8,128)}, u32[]{:S(2)}) copy-start(f32[256,256]{1,0:T(8,128)} %param.6) | copy-start | bytes 786436
  35.0 7.9 %copy-start.3 = (s32[256]{0:T(256)S(1)}, s32[256]{0:T(256)}, u32[]{:S(2)}) copy-start(s32[256]{0:T(256)} %param.7) | copy-start | bytes 3076
  35.0 110.0 %all-to-all-start = ((f32[21,16,32,128]{3,1,0,2:T(8,128)}), f32[21,16,32,128]{3,1,0,2:T(8,128)}, u32[]{:S(2)}, u32[]{:S(2)}) async-start(f32[21,16,32,128]{3,1,0,2:T(8,128)} %fusion.2), calls=%async_computation | async-start | bytes 11010048 | tf_op jit(solution)/shard_map/all_to_all | solution.py:96
  157.3 0.7 copy-start.4
  158.7 27.6 %copy-start.5 = (s32[256]{0:T(256)S(1)}, s32[256]{0:T(256)}, u32[]{:S(2)}) copy-start(s32[256]{0:T(256)} %param.8) | copy-start | bytes 3076
  160.8 84.1 %all-to-all-start.1 = ((f32[6,256,2,128]{3,2,0,1:T(2,128)}), f32[6,256,2,128]{3,2,0,1:T(2,128)S(1)}, u32[]{:S(2)}, u32[]{:S(2)}) async-start(f32[6,256,2,128]{3,2,0,1:T(2,128)} %copy.31), calls=%async_computation.1 | async-start | bytes 3145728 | tf_op jit(solution)/shard_map/all_to_all | solution.py:106
  243.8 1.4 copy-start.6
where the time goes:
time: 247 us
  waiting for transfers between devices  107 us (43%)
  blocking collectives  56.8 us (23%)
  starting transfers between devices  40 us (16%)
  other arithmetic  18.2 us (7%)
  local copies, waits for them, and re-layouts  14 us (6%)
  matrix products  9.47 us (4%)
    all_to_all x1, waiting for transfers between devices, local(): lax.all_to_all(boxed, 'pz', split_axis=2, concat_axis=1, tiled=True)  102 us
    psum x1, blocking collectives, local(): numer, denom = lax.psum((local_lm, local_mm), ('px', 'pz'))  56.8 us
    all_to_all x1, starting transfers between devices, local(): lax.all_to_all(leonard, 'pz', split_axis=1, concat_axis=2, tiled=True)  25.5 us
    dot_general x1, matrix products, local(): jnp.einsum('ab,kbzx->kazx', weights, smooth_boxed, precision=lax.Precisio...  8.81 us
    all_to_all x1, starting transfers between devices, local(): lax.all_to_all(boxed, 'pz', split_axis=2, concat_axis=1, tiled=True)  7.84 us
    ppermute x2, starting transfers between devices, with_halo(): lax.ppermute(tail, axis, [(i, (i + 1) % count) for i in range(ends)])  5.12 us
  transfers between devices with their start and end apart: 6, of which 4 were waited for; matrix products, arithmetic and copies ran while one was open for 1% of the time, Pallas kernels for 0%

commit v1 on v0

--- a/solution.py
+++ b/solution.py
@@ -103,7 +103,9 @@
     cells = filtered.shape[3] * lax.axis_size("px") * filtered.shape[2] * lax.axis_size("pz")
     per_bin = numer / jnp.maximum(denom, jnp.float32(cells))
     coefficient = jnp.dot(onehot, per_bin, precision=lax.Precision.HIGHEST)
-    leonard_back = lax.all_to_all(leonard, "pz", split_axis=1, concat_axis=2, tiled=True)
+    parts = jnp.split(leonard, lax.axis_size("pz"), axis=1)
+    incoming = lax.all_to_all(jnp.stack(parts), "pz", 0, 0)
+    leonard_back = jnp.concatenate(incoming, axis=2)
     offset = lax.axis_index("pz") * local_planes
     local_coef = lax.dynamic_slice_in_dim(coefficient, offset, local_planes, 0)
     viscosity = local_coef[:, None, None] * magnitude

time: 247 us -> 289 us (1.17)
  local copies, waits for them, and re-layouts: 14 us -> 54.6 us
    another operation x0 -> x18, local copies, waits for them, and re-layouts: none -> 31.9 us  [local(): incoming = lax.all_to_all(jnp.stack(parts), 'pz', 0, 0)]
    unnamed x21 -> x52, local copies, waits for them, and re-layouts: 4.01 us -> 16 us
where the time goes in v1:
time: 289 us; the launch traced here: 288 us
  waiting for transfers between devices  107 us (37%)
  blocking collectives  56.8 us (20%)
  local copies, waits for them, and re-layouts  54.6 us (19%)
  starting transfers between devices  40.2 us (14%)
  other arithmetic  18.2 us (6%)
  matrix products  9.47 us (3%)
    all_to_all x1, waiting for transfers between devices, local(): lax.all_to_all(boxed, 'pz', split_axis=2, concat_axis=1, tiled=True)  102 us
    psum x1, blocking collectives, local(): numer, denom = lax.psum((local_lm, local_mm), ('px', 'pz'))  56.8 us
    another operation x18, local copies, waits for them, and re-layouts, local(): incoming = lax.all_to_all(jnp.stack(parts), 'pz', 0, 0)  31.9 us
    all_to_all x1, starting transfers between devices, local(): incoming = lax.all_to_all(jnp.stack(parts), 'pz', 0, 0)  25.5 us
    unnamed x52, local copies, waits for them, and re-layouts  16 us
    dot_general x1, matrix products, local(): jnp.einsum('ab,kbzx->kazx', weights, smooth_boxed, precision=lax.Precisio...  8.81 us
    all_to_all x1, starting transfers between devices, local(): lax.all_to_all(boxed, 'pz', split_axis=2, concat_axis=1, tiled=True)  8.05 us
  transfers between devices with their start and end apart: 6, of which 4 were waited for; matrix products, arithmetic and copies ran while one was open for 1% of the time, Pallas kernels for 0%

profile of v1, /device:TPU:0, one launch (start us, length us, event | category | flops | bytes accessed | tf_op | source)
XLA Modules:
  0.0 287.6 jit_solution(6737788298393811100)
XLA Ops:
  0.6 1.7 fusion.38
  5.3 0.7 pad_maximum_fusion.18
  6.0 4.6 %collective-permute-start.2 = (f32[3,1,32,132]{3,1,0,2:T(1,128)S(1)}, f32[3,1,32,132]{3,1,0,2:T(1,128)S(1)}, u32[]{:S(2)}, u32[]{:S(2)}) collective-permute-start(f32[3,1,32,132]{3,1,0,2:T(1,128)S(1)} %get-tuple-element.30), channel_id=1, source_target_pairs={{0,1},{1,2},{2,3},{3,4},{4,5},{5,6},{6,7},{7,8},{8,9},{9,10},{10,1... | collective-permute-start | bytes 152072 | tf_op jit(solution)/shard_map/ppermute | solution.py:17
  10.6 1.5 collective-permute-start.3
  12.1 1.0 collective-permute-done.2
  13.1 4.1 %collective-permute-done.3 = f32[3,1,32,132]{3,1,0,2:T(1,128)S(1)} collective-permute-done((f32[3,1,32,132]{3,1,0,2:T(1,128)S(1)}, f32[3,1,32,132]{3,1,0,2:T(1,128)S(1)}, u32[]{:S(2)}, u32[]{:S(2)}) %collective-permute-start.3) | collective-permute-done | bytes 50720 | tf_op jit(solution)/shard_map/ppermute | solution.py:19
  17.4 1.0 pad_maximum_fusion
  18.5 3.0 %fusion.6 = (f32[3,16,34,130]{3,1,0,2:T(8,128)}, f32[3,16,34,130]{3,1,0,2:T(8,128)S(1)}, f32[21,16,34,130]{3,1,0,2:T(8,128)S(1)}) fusion(f32[3,18,36,132]{3,1,0,2:T(8,128)S(1)} %pad_maximum_fusion), kind=kLoop, calls=%fused_computation.25 | loop fusion | flops 848639 | bytes 8434176 | tf_op jit(solution)/shard_map/mul | solution.py:28
  21.6 1.3 copy-done.1
  23.1 2.1 fusion.5
  28.9 3.2 %fusion = f32[21,16,34,128]{3,1,0,2:T(8,128)S(1)} fusion(f32[21,16,34,130]{3,1,0,2:T(8,128)S(1)} %multiply_dynamic-update-slice_fusion), kind=kLoop, calls=%fused_computation.1 | loop fusion | flops 5849088 | bytes 23396352 | tf_op jit(solution)/shard_map/mul | solution.py:56
  32.1 3.1 %fusion.2 = f32[21,16,32,128]{3,1,0,2:T(8,128)} fusion(f32[21,16,34,128]{3,1,0,2:T(8,128)S(1)} %fusion), kind=kLoop, calls=%fused_computation.5 | loop fusion | flops 5505024 | bytes 22020096 | tf_op jit(solution)/shard_map/mul | solution.py:57
  35.2 8.0 %all-to-all-start = ((f32[21,16,32,128]{3,1,0,2:T(8,128)}), f32[21,16,32,128]{3,1,0,2:T(8,128)}, u32[]{:S(2)}, u32[]{:S(2)}) async-start(f32[21,16,32,128]{3,1,0,2:T(8,128)} %fusion.2), calls=%async_computation | async-start | bytes 11010048 | tf_op jit(solution)/shard_map/all_to_all | solution.py:96
  43.5 101.8 %all-to-all-done = f32[21,16,32,128]{3,1,0,2:T(8,128)} async-done(((f32[21,16,32,128]{3,1,0,2:T(8,128)}), f32[21,16,32,128]{3,1,0,2:T(8,128)}, u32[]{:S(2)}, u32[]{:S(2)}) %all-to-all-start) | async-done | bytes 5505056 | tf_op jit(solution)/shard_map/all_to_all | solution.py:96
  145.3 3.3 %copy.28 = f32[21,16,16,2,128]{4,2,1,3,0:T(8,128)S(1)} copy(f32[21,16,16,2,128]{4,2,0,3,1:T(8,128)} %bitcast.2) | data formatting | bytes 11010048 | tf_op jit(solution)/shard_map/all_to_all | solution.py:96
  148.6 8.8 %convolution_bitcast_fusion = f32[21,256,2,128]{1,3,2,0:T(8,128)S(1)} fusion(f32[21,256,2,128]{3,1,2,0:T(8,128)S(1)} %bitcast.59, f32[256,256]{1,0:T(8,128)S(1)} %copy-done.2, f32[256]{0:T(256)S(1)} %fusion.19, s32[256]{0:T(256)S(1)} %copy-done.11), kind=kOutput, calls=%fused_computation.10 | convolution fusion | flops 4228055040 | bytes 11274240 | tf_op jit(solution)/shard_map/ab,kbzx->kazx/dot_general | solution.py:97
  158.3 0.8 fusion.10
  159.1 7.0 %slice_bitcast_fusion = (f32[1,6,16,2,128]{2,4,3,1,0:T(8,128)}, f32[1,6,16,2,128]{2,4,3,1,0:T(8,128)}, f32[1,6,16,2,128]{2,4,3,1,0:T(8,128)}, f32[1,6,16,2,128]{...) fusion(f32[6,256,2,128]{1,3,2,0:T(8,128)S(1)} %get-tuple-element.18), kind=kLoop, calls=%fused_computation.44 | loop fusion | bytes 3145728 | tf_op jit(solution)/shard_map/stack | solution.py:107
  166.1 1.4 copy.45
  167.5 1.4 copy.44
  168.9 1.4 copy.43
  170.2 1.4 copy.42
  171.6 1.4 copy.41
  173.0 1.4 copy.40
  174.3 2.0 copy.39
  176.4 2.0 copy.38
  178.4 2.0 copy.37
  180.4 2.0 copy.36
  182.4 2.0 copy.35
  184.4 2.0 copy.34
  186.4 2.0 copy.33
  188.4 0.9 copy.32
  189.3 0.9 copy.31
  190.4 0.7 constant_dynamic-update-slice_fusion.27
  191.1 1.5 constant_dynamic-update-slice_fusion.26
  192.6 0.6 constant_dynamic-update-slice_fusion.25
  193.3 0.6 constant_dynamic-update-slice_fusion.24
  193.9 0.6 constant_dynamic-update-slice_fusion.23
  194.6 0.6 constant_dynamic-update-slice_fusion.22
  195.2 0.6 constant_dynamic-update-slice_fusion.21
  195.9 0.6 constant_dynamic-update-slice_fusion.20
  196.5 0.6 constant_dynamic-update-slice_fusion.19
  197.2 0.6 constant_dynamic-update-slice_fusion.18
  199.8 0.6 constant_dynamic-update-slice_fusion.14
  201.7 25.5 %all-to-all-start.1 = ((f32[16,6,16,2,128]{4,2,3,1,0:T(8,128)}), f32[16,6,16,2,128]{4,2,3,1,0:T(8,128)S(1)}, u32[]{:S(2)}, u32[]{:S(2)}) async-start(f32[16,6,16,2,128]{4,2,3,1,0:T(8,128)} %constant_dynamic-update-slice_fusion.12), calls=%async_computation.1 | async-start | bytes 3145728 | tf_op jit(solution)/shard_map/all_to_all | solution.py:107
  227.7 56.8 %all-reduce = (f32[64]{0:T(128)S(1)}, f32[64]{0:T(128)S(1)}) all-reduce(f32[64]{0:T(128)S(1)} %convolution_bitcast_fusion.2, f32[64]{0:T(128)S(1)} %convolution_bitcast_fusion.1), channel_id=1, replica_groups=mesh['px'=2,'pz'=16] {'px','pz'}, use_global_device_ids=true, to_apply=%region_6.0 | all-reduce | flops 128 | bytes 1024 | tf_op jit(solution)/shard_map/psum | solution.py:102
  285.0 0.8 copy.48
  286.0 1.6 copy.47
  (79 shorter events, 12.6 us)
Async XLA Ops:
  0.6 3.1 %copy-start = (f32[3,16,32,128]{3,2,1,0:T(8,128)S(1)}, f32[3,16,32,128]{3,2,1,0:T(8,128)}, u32[]{:S(2)}) copy-start(f32[3,16,32,128]{3,2,1,0:T(8,128)} %param.5) | copy-start | bytes 2359300
  2.7 1.4 collective-permute-start
  3.6 1.3 collective-permute-start.1
  6.0 7.1 %collective-permute-start.2 = (f32[3,1,32,132]{3,1,0,2:T(1,128)S(1)}, f32[3,1,32,132]{3,1,0,2:T(1,128)S(1)}, u32[]{:S(2)}, u32[]{:S(2)}) collective-permute-start(f32[3,1,32,132]{3,1,0,2:T(1,128)S(1)} %get-tuple-element.30), channel_id=1, source_target_pairs={{0,1},{1,2},{2,3},{3,4},{4,5},{5,6},{6,7},{7,8},{8,9},{9,10},{10,1... | collective-permute-start | bytes 152072 | tf_op jit(solution)/shard_map/ppermute | solution.py:17
  10.6 6.6 %collective-permute-start.3 = (f32[3,1,32,132]{3,1,0,2:T(1,128)S(1)}, f32[3,1,32,132]{3,1,0,2:T(1,128)S(1)}, u32[]{:S(2)}, u32[]{:S(2)}) collective-permute-start(f32[3,1,32,132]{3,1,0,2:T(1,128)S(1)} %get-tuple-element.31), channel_id=1, source_target_pairs={{1,0},{2,1},{3,2},{4,3},{5,4},{6,5},{7,6},{8,7},{9,8},{10,9},{11,1... | collective-permute-start | bytes 152072 | tf_op jit(solution)/shard_map/ppermute | solution.py:19
  21.5 1.4 copy-start.1
  35.2 8.1 %copy-start.2 = (f32[256,256]{1,0:T(8,128)S(1)}, f32[256,256]{1,0:T(8,128)}, u32[]{:S(2)}) copy-start(f32[256,256]{1,0:T(8,128)} %param.6) | copy-start | bytes 786436
  35.2 8.1 %copy-start.11 = (s32[256]{0:T(256)S(1)}, s32[256]{0:T(256)}, u32[]{:S(2)}) copy-start(s32[256]{0:T(256)} %param.7) | copy-start | bytes 3076
  35.2 110.0 %all-to-all-start = ((f32[21,16,32,128]{3,1,0,2:T(8,128)}), f32[21,16,32,128]{3,1,0,2:T(8,128)}, u32[]{:S(2)}, u32[]{:S(2)}) async-start(f32[21,16,32,128]{3,1,0,2:T(8,128)} %fusion.2), calls=%async_computation | async-start | bytes 11010048 | tf_op jit(solution)/shard_map/all_to_all | solution.py:96
  157.6 0.7 copy-start.12
  189.3 3.4 %copy-start.10 = (f32[1,6,16,2,128]{4,2,3,1,0:T(8,128)S(1)}, f32[1,6,16,2,128]{4,2,3,1,0:T(8,128)}, u32[]{:S(2)}) copy-start(f32[1,6,16,2,128]{4,2,3,1,0:T(8,128)} %copy.32) | copy-start | bytes 294916
  189.3 4.0 %copy-start.9 = (f32[1,6,16,2,128]{4,2,3,1,0:T(8,128)S(1)}, f32[1,6,16,2,128]{4,2,3,1,0:T(8,128)}, u32[]{:S(2)}) copy-start(f32[1,6,16,2,128]{4,2,3,1,0:T(8,128)} %copy.33) | copy-start | bytes 294916
  189.3 4.7 %copy-start.8 = (f32[1,6,16,2,128]{4,2,3,1,0:T(8,128)S(1)}, f32[1,6,16,2,128]{4,2,3,1,0:T(8,128)}, u32[]{:S(2)}) copy-start(f32[1,6,16,2,128]{4,2,3,1,0:T(8,128)} %copy.34) | copy-start | bytes 294916
  189.3 5.3 %copy-start.7 = (f32[1,6,16,2,128]{4,2,3,1,0:T(8,128)S(1)}, f32[1,6,16,2,128]{4,2,3,1,0:T(8,128)}, u32[]{:S(2)}) copy-start(f32[1,6,16,2,128]{4,2,3,1,0:T(8,128)} %copy.35) | copy-start | bytes 294916
  189.3 6.0 %copy-start.6 = (f32[1,6,16,2,128]{4,2,3,1,0:T(8,128)S(1)}, f32[1,6,16,2,128]{4,2,3,1,0:T(8,128)}, u32[]{:S(2)}) copy-start(f32[1,6,16,2,128]{4,2,3,1,0:T(8,128)} %copy.36) | copy-start | bytes 294916
  189.3 6.6 %copy-start.5 = (f32[1,6,16,2,128]{4,2,3,1,0:T(8,128)S(1)}, f32[1,6,16,2,128]{4,2,3,1,0:T(8,128)}, u32[]{:S(2)}) copy-start(f32[1,6,16,2,128]{4,2,3,1,0:T(8,128)} %copy.37) | copy-start | bytes 294916
  189.3 7.2 %copy-start.4 = (f32[1,6,16,2,128]{4,2,3,1,0:T(8,128)S(1)}, f32[1,6,16,2,128]{4,2,3,1,0:T(8,128)}, u32[]{:S(2)}) copy-start(f32[1,6,16,2,128]{4,2,3,1,0:T(8,128)} %copy.38) | copy-start | bytes 294916
  189.3 7.9 %copy-start.3 = (f32[1,6,16,2,128]{4,2,3,1,0:T(8,128)S(1)}, f32[1,6,16,2,128]{4,2,3,1,0:T(8,128)}, u32[]{:S(2)}) copy-start(f32[1,6,16,2,128]{4,2,3,1,0:T(8,128)} %copy.39) | copy-start | bytes 294916
  201.1 26.1 %copy-start.13 = (s32[256]{0:T(256)S(1)}, s32[256]{0:T(256)}, u32[]{:S(2)}) copy-start(s32[256]{0:T(256)} %param.8) | copy-start | bytes 3076
  201.7 84.1 %all-to-all-start.1 = ((f32[16,6,16,2,128]{4,2,3,1,0:T(8,128)}), f32[16,6,16,2,128]{4,2,3,1,0:T(8,128)S(1)}, u32[]{:S(2)}, u32[]{:S(2)}) async-start(f32[16,6,16,2,128]{4,2,3,1,0:T(8,128)} %constant_dynamic-update-slice_fusion.12), calls=%async_computation.1 | async-start | bytes 3145728 | tf_op jit(solution)/shard_map/all_to_all | solution.py:107
  284.7 1.2 copy-start.14
